TPU v7x, 32 devices: a whole 2x2x4 slice. The times are simulated.
32 devices in a mesh: tile: 8 (over z, y), rep: 4 (over x, core).
Axes of the slice: x: 2, y: 2, z: 4, core: 2. Of those that a mesh axis runs over, the one named last changes fastest.
Arguments:
- amplitudes: bfloat16 [1024, 8192], P(None, ('tile', 'rep')), may hold values from -3 to 3
- integrals: bfloat16 [4, 512, 128, 128], P('rep', 'tile'), may hold values from -0.1875 to 0.1875
- slot_row: int32 [4, 512], P('rep', 'tile'), may hold values from 0 to 7, as said below
- slot_col: int32 [4, 512], P('rep', 'tile'), may hold values from 0 to 15
- slot_count: int32 [4, 8], P('rep', 'tile'), may hold values from 32 to 64, as said below
- source: float32 [1024, 8192], P(None, ('tile', 'rep')), may hold values from -6 to 6
- occ_energy: float32 [1024], replicated, may hold values from -2 to -0.4
- virt_energy: float32 [8192], P(('tile', 'rep')), may hold values from 0.5 to 6.5
Outputs:
- residual: float32 [1024, 8192], P(None, ('tile', 'rep'))
- updated: float32 [1024, 8192], P(None, ('tile', 'rep'))
Inputs may be any that keep to these rules, and one draw needn't show every extreme that they name: `slot_row`: within one device's 64 slots no pair of row tile and contraction tile occurs twice. `slot_count`: some device has all 64 slots live.
All inputs are finite; a program needn't handle non-finite values.
Results may differ from a plain program's by a relative error of at most 0.0003.
Values may be sent and summed in bfloat16 or wider, within the bound.
A program may use at most 128 MiB of HBM per device.

v0:
```python
import math

import jax
import jax.numpy as jnp
from jax import lax
from jax.sharding import PartitionSpec as P

BT = 128
PT_DEV = 8


slot_block = 16
trust = 0.1


def slot_terms(tiles, ints, rows, cols, first, last):
    opairs = tiles.shape[0]
    edge = tiles.shape[2]
    block = math.gcd(slot_block, ints.shape[0])
    row_tiles = PT_DEV

    def add_block(index, total):
        start = (index * block).astype(jnp.int32)
        vblock = lax.dynamic_slice_in_dim(ints, start, block, 0)
        rblock = lax.dynamic_slice_in_dim(rows, start, block, 0)
        cblock = lax.dynamic_slice_in_dim(cols, start, block, 0)
        picked = jnp.take(tiles, cblock, axis=1)
        terms = jnp.einsum("osc,sec->soe", picked, vblock, preferred_element_type=jnp.float32)
        where = start + lax.iota(jnp.int32, block)
        live = (where >= first) & (where < last)
        select = (
            (rblock[:, None] == lax.iota(jnp.int32, row_tiles)[None, :]) & live[:, None]
        ).astype(jnp.float32)
        return total + jnp.einsum("sk,soe->oke", select, terms, precision=lax.Precision.HIGHEST)

    total = jnp.zeros((opairs, row_tiles, edge), jnp.float32)
    lower = first // block
    upper = jnp.maximum((last + block - 1) // block, lower)
    total = lax.fori_loop(lower, upper, add_block, total)
    return total.reshape(opairs, row_tiles * edge)


def local(amplitudes, integrals, slot_row, slot_col, slot_count, source, occ_energy, virt_energy):
    gathered = lax.all_gather(amplitudes, "tile", axis=1, tiled=True)
    opairs = gathered.shape[0]
    tiles = gathered.reshape(opairs, gathered.shape[1] // BT, BT)
    ints = integrals[0]
    rows = slot_row[0]
    cols = slot_col[0]
    count = slot_count[0, 0]
    partial_value = slot_terms(tiles, ints, rows, cols, jnp.int32(0), count)
    residual = source + lax.psum_scatter(partial_value, "rep", scatter_dimension=1, tiled=True)
    step = residual / (virt_energy[None, :] - occ_energy[:, None])
    total_sq = lax.psum(jnp.sum(step * step), ("tile", "rep"))
    entries = opairs * virt_energy.shape[0] * lax.axis_size("tile") * lax.axis_size("rep")
    scale = jnp.minimum(1.0, trust / jnp.sqrt(total_sq / entries + 1e-06))
    updated = amplitudes.astype(jnp.float32) + scale * step
    return (residual, updated)


def solution(mesh):
    placed = (
        P(None, ("tile", "rep")),
        P("rep", "tile", None, None),
        P("rep", "tile"),
        P("rep", "tile"),
        P("rep", "tile"),
        P(None, ("tile", "rep")),
        P(),
        P(("tile", "rep")),
    )
    return jax.shard_map(
        local,
        mesh=mesh,
        in_specs=placed,
        out_specs=(P(None, ("tile", "rep")), P(None, ("tile", "rep"))),
        check_vma=False,
    )
```

profile of v0, /device:TPU:0, one launch (start us, length us, event | category | flops | bytes accessed | tf_op | source)
XLA Modules:
  0.0 285.0 jit_solution(15145059734900306652)
XLA Ops:
  7.2 0.0 all-gather.2.cloned.1.call-start
  7.2 2.0 copy.11
  9.3 0.0 all-gather.2.cloned.1.call-update
  9.3 0.0 reduce-scatter.2.cloned.1.call-start
  10.0 76.2 %all-gather.2.cloned.1.call-done = bf16[1024,2048]{0,1:T(8,128)(2,1)} async-done(((bf16[1024,256]{0,1:T(8,128)(2,1)}), bf16[1024,2048]{0,1:T(8,128)(2,1)}) %all-gather.2.cloned.1.call-update) | async-done | bytes 4194320 | tf_op jit(solution)/shard_map/all_gather | solution.py:44
  86.2 6.4 %copy.12 = bf16[1024,16,128]{2,0,1:T(8,128)(2,1)} copy(bf16[1024,16,128]{0,2,1:T(8,128)(2,1)} %bitcast.25) | data formatting | bytes 8388608 | tf_op jit(solution)/shard_map/while | solution.py:39
  92.6 0.0 copy-start.4
  92.6 0.0 copy-start.6
  92.6 2.3 broadcast_in_dim.20
  94.9 0.0 copy-done.4
  94.9 0.0 copy-done.6
  94.9 68.6 %while.10 = (s32[]{:T(128)}, f32[1024,8,128]{2,1,0:T(8,128)}, s32[]{:T(128)}, s32[64]{0:T(128)S(1)}, bf16[1024,16,128]{2,0,1:T(8,128)(2,1)}, /*index=5*/bf16[64,...) while((s32[]{:T(128)}, f32[1024,8,128]{2,1,0:T(8,128)}, ...), condition=%wide.region_1.2_spmd, body=%wide.region_0.1_spmd.sunk | while | flops 741344704 | bytes 38277816 | solution.py:39
  94.9 0.7 compare_and_fusion.3
  95.6 5.2 %gather_fusion = bf16[16,1024,128]{2,1,0:T(8,128)(2,1)} fusion(bf16[1024,16,128]{2,0,1:T(8,128)(2,1)} %get-tuple-element.159, s32[1024]{0:T(1024)S(1)} %pad_clamp_fusion.2), kind=kCustom, calls=%fused_computation.clone.1 | custom fusion | bytes 8388672 | tf_op jit(solution)/shard_map/while/body/jit(_take)/gather | solution.py:27
  100.8 3.6 %fusion.26 = f32[16,1024,128]{2,1,0:T(8,128)S(1)} fusion(bf16[16,1024,128]{2,1,0:T(8,128)(2,1)} %gather_fusion, pred[16]{0:T(512)(128)(4,1)S(1)} %get-tuple-element.129, bf16[64,128,128]{2,1,0:T(8,128)(2,1)} %get-tuple-element.160, s32[]{:T(128)S(6)} %select_n.31), kind=kOutput, calls=%fused_computation.4.clone.1 | convolution fusion | flops 538968064 | bytes 13107220 | tf_op jit(solution)/shard_map/while/body/osc,sec->soe/dot_general | solution.py:28
  104.4 0.1 dynamic_slice.16
  104.5 13.2 %bitcast_add_fusion.2 = f32[1024,8,128]{2,1,0:T(8,128)} fusion(f32[1024,8,128]{2,1,0:T(8,128)} %get-tuple-element.144, f32[16,1024,128]{2,1,0:T(8,128)S(1)} %fusion.26, s32[16]{0:T(128)S(1)} %dynamic_slice.16, pred[16]{0:T(512)(128)(4,1)S(1)} %get-tuple-element.130), kind=kOutput, calls=%fused_computation.3.clone.1 | convolution fusion | flops 202375424 | bytes 16777296 | tf_op jit(solution)/shard_map/while/body/sk,soe->oke/dot_general | solution.py:34
  117.7 0.7 compare_and_fusion.3
  118.5 5.2 %gather_fusion = bf16[16,1024,128]{2,1,0:T(8,128)(2,1)} fusion(bf16[1024,16,128]{2,0,1:T(8,128)(2,1)} %get-tuple-element.159, s32[1024]{0:T(1024)S(1)} %pad_clamp_fusion.2), kind=kCustom, calls=%fused_computation.clone.1 | custom fusion | bytes 8388672 | tf_op jit(solution)/shard_map/while/body/jit(_take)/gather | solution.py:27
  123.7 3.6 %fusion.26 = f32[16,1024,128]{2,1,0:T(8,128)S(1)} fusion(bf16[16,1024,128]{2,1,0:T(8,128)(2,1)} %gather_fusion, pred[16]{0:T(512)(128)(4,1)S(1)} %get-tuple-element.129, bf16[64,128,128]{2,1,0:T(8,128)(2,1)} %get-tuple-element.160, s32[]{:T(128)S(6)} %select_n.31), kind=kOutput, calls=%fused_computation.4.clone.1 | convolution fusion | flops 538968064 | bytes 13107220 | tf_op jit(solution)/shard_map/while/body/osc,sec->soe/dot_general | solution.py:28
  127.3 0.1 dynamic_slice.16
  127.4 13.2 %bitcast_add_fusion.2 = f32[1024,8,128]{2,1,0:T(8,128)} fusion(f32[1024,8,128]{2,1,0:T(8,128)} %get-tuple-element.144, f32[16,1024,128]{2,1,0:T(8,128)S(1)} %fusion.26, s32[16]{0:T(128)S(1)} %dynamic_slice.16, pred[16]{0:T(512)(128)(4,1)S(1)} %get-tuple-element.130), kind=kOutput, calls=%fused_computation.3.clone.1 | convolution fusion | flops 202375424 | bytes 16777296 | tf_op jit(solution)/shard_map/while/body/sk,soe->oke/dot_general | solution.py:34
  140.6 0.7 compare_and_fusion.3
  141.3 5.2 %gather_fusion = bf16[16,1024,128]{2,1,0:T(8,128)(2,1)} fusion(bf16[1024,16,128]{2,0,1:T(8,128)(2,1)} %get-tuple-element.159, s32[1024]{0:T(1024)S(1)} %pad_clamp_fusion.2), kind=kCustom, calls=%fused_computation.clone.1 | custom fusion | bytes 8388672 | tf_op jit(solution)/shard_map/while/body/jit(_take)/gather | solution.py:27
  146.6 3.6 %fusion.26 = f32[16,1024,128]{2,1,0:T(8,128)S(1)} fusion(bf16[16,1024,128]{2,1,0:T(8,128)(2,1)} %gather_fusion, pred[16]{0:T(512)(128)(4,1)S(1)} %get-tuple-element.129, bf16[64,128,128]{2,1,0:T(8,128)(2,1)} %get-tuple-element.160, s32[]{:T(128)S(6)} %select_n.31), kind=kOutput, calls=%fused_computation.4.clone.1 | convolution fusion | flops 538968064 | bytes 13107220 | tf_op jit(solution)/shard_map/while/body/osc,sec->soe/dot_general | solution.py:28
  150.2 0.1 dynamic_slice.16
  150.2 13.2 %bitcast_add_fusion.2 = f32[1024,8,128]{2,1,0:T(8,128)} fusion(f32[1024,8,128]{2,1,0:T(8,128)} %get-tuple-element.144, f32[16,1024,128]{2,1,0:T(8,128)S(1)} %fusion.26, s32[16]{0:T(128)S(1)} %dynamic_slice.16, pred[16]{0:T(512)(128)(4,1)S(1)} %get-tuple-element.130), kind=kOutput, calls=%fused_computation.3.clone.1 | convolution fusion | flops 202375424 | bytes 16777296 | tf_op jit(solution)/shard_map/while/body/sk,soe->oke/dot_general | solution.py:34
  163.4 5.1 %copy.19 = f32[128,8,8,128]{3,1,2,0:T(8,128)} copy(f32[128,8,8,128]{3,2,1,0:T(8,128)} %bitcast.8) | data formatting | bytes 8388608
  168.6 0.0 copy-start.2
  168.6 0.0 copy-start.3
  168.6 0.0 copy-start.5
  168.6 0.0 copy-start.1
  168.6 0.0 reduce-scatter.2.cloned.1.call-update
  168.6 65.9 %reduce-scatter.2.cloned.1.call-done = f32[1024,256]{1,0:T(8,128)} async-done(((f32[1024,1024]{1,0:T(8,128)}), f32[1024,256]{1,0:T(8,128)}) %reduce-scatter.2.cloned.1.call-update) | async-done | bytes 1048592 | tf_op jit(solution)/shard_map/reduce_scatter | solution.py:52
  234.6 0.0 copy-done.2
  234.6 0.0 copy-done.3
  234.6 0.0 copy-done.5
  234.6 2.2 multiply_reduce_fusion
  236.8 0.0 copy-start
  236.8 39.4 %psum.7 = f32[]{:T(128)} all-reduce(f32[]{:T(128)} %get-tuple-element.72), channel_id=1, replica_groups=mesh['tile'=8,'rep'=4] {'tile','rep'}, use_global_device_ids=true, to_apply=%region_4.5 | all-reduce | flops 1 | bytes 8 | tf_op jit(solution)/shard_map/psum | solution.py:54
  276.9 0.0 copy-done.1
  276.9 1.3 multiply_add_fusion
  278.2 0.0 copy-done
  (3 shorter events, 0.0 us)
Async XLA Ops:
  7.2 79.1 %all-gather.2.cloned.1.call-start = ((), (), s32[]{:S(2)}) async-start(), calls=%async_computation.1 | async-start | bytes 4718592 | tf_op jit(solution)/shard_map/all_gather | solution.py:44
  9.3 225.3 %reduce-scatter.2.cloned.1.call-start = ((), (), s32[]{:S(2)}) async-start(), calls=%async_computation.2 | async-start | bytes 5242880 | tf_op jit(solution)/shard_map/reduce_scatter | solution.py:52
  92.6 2.3 copy-start.4
  92.6 2.3 copy-start.6
  168.6 66.0 %copy-start.2 = (f32[1024,256]{1,0:T(8,128)S(1)}, f32[1024,256]{1,0:T(8,128)}, u32[]{:S(2)}) copy-start(f32[1024,256]{1,0:T(8,128)} %param.15) | copy-start | bytes 3145732
  168.6 66.0 %copy-start.3 = (f32[1024]{0:T(1024)S(1)}, f32[1024]{0:T(1024)}, u32[]{:S(2)}) copy-start(f32[1024]{0:T(1024)} %param.16) | copy-start | bytes 12292
  168.6 66.0 %copy-start.5 = (f32[256]{0:T(256)S(1)}, f32[256]{0:T(256)}, u32[]{:S(2)}) copy-start(f32[256]{0:T(256)} %param.17) | copy-start | bytes 3076
  168.6 108.3 %copy-start.1 = (bf16[1024,256]{1,0:T(8,128)(2,1)S(1)}, bf16[1024,256]{1,0:T(8,128)(2,1)}, u32[]{:S(2)}) copy-start(bf16[1024,256]{1,0:T(8,128)(2,1)} %param.10) | copy-start | bytes 1572868
  236.8 41.4 %copy-start = (f32[1024,256]{1,0:T(8,128)}, f32[1024,256]{1,0:T(8,128)S(1)}, u32[]{:S(2)}) copy-start(f32[1024,256]{1,0:T(8,128)S(1)} %get-tuple-element.73) | copy-start | bytes 3145732
Sparse Core Ops, SparseCore 0:
  10.7 75.5 all-gather.1
  168.7 65.7 reduce-scatter.1
where the time goes:
time: 286 us; the launch traced here: 285 us
  waiting for transfers between devices  142 us (50%)
  matrix products  50.4 us (18%)
  blocking collectives  39.4 us (14%)
  local copies, waits for them, and re-layouts  31.8 us (11%)
  between operations  15.4 us (5%)
  other arithmetic  5.65 us (2%)
    all_gather x1, waiting for transfers between devices, local(): gathered = lax.all_gather(amplitudes, 'tile', axis=1, tiled=True)  76.2 us
    reduce_scatter x1, waiting for transfers between devices, local(): lax.psum_scatter(partial_value, 'rep', scatter_dimension=1, tiled=True)  65.9 us
    dot_general x3, matrix products, add_block(): jnp.einsum('sk,soe->oke', select, terms, precision=lax.Precision.HIGHEST)  39.6 us
    psum x1, blocking collectives, local(): total_sq = lax.psum(jnp.sum(step * step), ('tile', 'rep'))  39.4 us
    gather x3, local copies, waits for them, and re-layouts, add_block(): picked = jnp.take(tiles, cblock, axis=1)  15.7 us
    dot_general x3, matrix products, add_block(): jnp.einsum('osc,sec->soe', picked, vblock, preferred_element_type=jnp.flo...  10.8 us
    unnamed x16, local copies, waits for them, and re-layouts  7.2 us
    while x1, local copies, waits for them, and re-layouts, slot_terms(): total = lax.fori_loop(lower, upper, add_block, total)  6.38 us
  transfers between devices with their start and end apart: 2, of which 2 were waited for; matrix products, arithmetic and copies ran while one was open for 0% of the time, Pallas kernels for 0%

commit v1 on v0

v1 whole, which is shorter than its diff:
```python
import functools

import jax
import jax.numpy as jnp
from jax import lax
from jax.experimental import pallas as pl
from jax.experimental.pallas import tpu as pltpu
from jax.sharding import PartitionSpec as P

BT = 128
PT_DEV = 8
trust = 0.1
CHUNKS = 16
AHEAD = 4
MESH = pl.DeviceIdType.MESH


def cross_chunk(j):
    return lax.rem(j, 5) == 2


def kernel(
    nt, nr, nc,
    amp, ints, row, col, cnt, src, occ, virt,
    res_out, upd_out,
    gat, tiles, dense, inv_v, inv_s, occ_col, give, keep, core_in, x_out, x_in, src_v, res_v, step_v,
    sq, stat_a, stat_b, mine,
    su, sd, sy, rg, ds_, dr, xs, xr, sas, sar, sbs, sbr, loc, rsem, usem,
):
    t = lax.axis_index("tile")
    r = lax.axis_index("rep")
    rows_all, cols = amp.shape
    rc = rows_all // nc
    nloc = ints.shape[1]
    line = nt // 2
    q = cols // BT
    qr = nt * q
    nh = nr // 2
    l = t // 2
    y = lax.rem(t, 2)
    h = r // 2
    c = lax.rem(r, 2)

    amp_in = pltpu.make_async_copy(amp, gat.at[t], loc.at[0])
    amp_in.start()
    ints_in = pltpu.make_async_copy(ints.at[0], tiles.at[pl.ds(0, nloc)], loc.at[1])
    ints_in.start()
    src_in = pltpu.make_async_copy(src, src_v, loc.at[2])
    src_in.start()

    barrier = pltpu.get_barrier_semaphore()
    for k in range(1, nt):
        pl.semaphore_signal(barrier, inc=1, device_id={"tile": lax.rem(t + k, nt)}, device_id_type=MESH)
    for k in range(1, nr):
        pl.semaphore_signal(barrier, inc=1, device_id={"rep": lax.rem(r + k, nr)}, device_id_type=MESH)
    pl.semaphore_wait(barrier, nt - 1 + nr - 1)

    def piece(source, j, sem, dest):
        ref = gat.at[source, pl.ds(pl.multiple_of(j * rc, rc), rc)]
        return pltpu.make_async_remote_copy(
            src_ref=ref, dst_ref=ref, send_sem=sem.at[source, j], recv_sem=rg.at[source, j],
            device_id={"tile": dest}, device_id_type=MESH,
        )

    up_to = lax.rem(t + 2, nt)
    down_to = lax.rem(t + nt - 2, nt)
    across = t + 1 - 2 * y

    def up(source, j):
        return piece(source, j, su, up_to)

    def down(source, j):
        return piece(source, j, sd, down_to)

    def side(source, j):
        return piece(source, j, sy, across)

    def send_own(j):
        side(t, j).start()

        @pl.when(l < line - 1)
        def _():
            up(t, j).start()

        @pl.when(l > 0)
        def _():
            down(t, j).start()

    amp_in.wait()
    for j in range(AHEAD):
        send_own(j)

    key = row[...] * qr + col[...]
    where = lax.broadcasted_iota(jnp.int32, (1, nloc), 1)
    key = jnp.where(where < cnt[...], key, -1)
    diag = lax.broadcasted_iota(jnp.int32, (nloc, nloc), 0) == lax.broadcasted_iota(jnp.int32, (nloc, nloc), 1)
    key_col = jnp.sum(jnp.where(diag, jnp.broadcast_to(key, (nloc, nloc)), 0), axis=1, keepdims=True)
    pairs = PT_DEV * qr
    hit = key_col == lax.broadcasted_iota(jnp.int32, (nloc, pairs), 1)
    slot = lax.broadcasted_iota(jnp.int32, (nloc, pairs), 0)
    found = nloc - jnp.sum(jnp.where(hit, nloc - slot, 0), axis=0, keepdims=True)
    inv_v[...] = jnp.broadcast_to(found, inv_v.shape)
    inv_in = pltpu.make_async_copy(inv_v, inv_s, loc.at[3])
    inv_in.start()

    sq[...] = jnp.zeros_like(sq)
    tiles[nloc] = jnp.zeros((BT, BT), tiles.dtype)
    eye = lax.broadcasted_iota(jnp.int32, (BT, BT), 0) == lax.broadcasted_iota(jnp.int32, (BT, BT), 1)
    for k in range(rows_all // BT):
        part = jnp.broadcast_to(occ[:, k * BT : (k + 1) * BT], (BT, BT))
        occ_col[k * BT : (k + 1) * BT, :] = jnp.sum(jnp.where(eye, part, 0.0), axis=1, keepdims=True)
    inv_in.wait()
    ints_in.wait()

    def build(b, carry):
        for k in range(PT_DEV):
            for m in range(q):
                at = inv_s[0, k * qr + b * q + m]
                dense[k * BT : (k + 1) * BT, pl.ds(pl.multiple_of(b * cols + m * BT, BT), BT)] = tiles[at]
        return carry

    lax.fori_loop(0, nt, build, 0)
    src_in.wait()

    def core_copy(j):
        return pltpu.make_async_remote_copy(
            src_ref=give.at[j], dst_ref=core_in.at[j], send_sem=ds_.at[j], recv_sem=dr.at[j],
            device_id={"rep": r + 1 - 2 * c}, device_id_type=MESH,
        )

    def x_copy(j, m):
        return pltpu.make_async_remote_copy(
            src_ref=x_out.at[j, m - 1], dst_ref=x_in.at[j, m - 1], send_sem=xs.at[j, m - 1], recv_sem=xr.at[j, m - 1],
            device_id={"rep": lax.rem(h + m, nh) * 2 + c}, device_id_type=MESH,
        )

    def res_copy(j):
        span = pl.ds(pl.multiple_of(j * rc, rc), rc)
        return pltpu.make_async_copy(res_v.at[span], res_out.at[span], rsem.at[j])

    latest = line

    def inside(j):
        return (j >= 0) & (j < nc)

    def forward(d, i):
        j = i - d + 1

        @pl.when(inside(j) & (d > 0))
        def _():
            @pl.when(l - d >= 0)
            def _():
                source = t - 2 * d
                up(source, j).wait_recv()

                @pl.when(l < line - 1)
                def _():
                    up(source, j).start()

                @pl.when(jnp.logical_not(cross_chunk(j)))
                def _():
                    side(source, j).start()

            @pl.when(l + d < line)
            def _():
                source = t + 2 * d
                down(source, j).wait_recv()

                @pl.when(l > 0)
                def _():
                    down(source, j).start()

                @pl.when(jnp.logical_not(cross_chunk(j)))
                def _():
                    side(source, j).start()

        m = i - d

        @pl.when(inside(m) & cross_chunk(m))
        def _():
            @pl.when(d == 0)
            def _():
                side(across, m).wait_recv()

                @pl.when(l < line - 1)
                def _():
                    up(across, m).start()

                @pl.when(l > 0)
                def _():
                    down(across, m).start()

            @pl.when((d > 0) & (l - d >= 0))
            def _():
                source = across - 2 * d
                up(source, m).wait_recv()

                @pl.when(l < line - 1)
                def _():
                    up(source, m).start()

            @pl.when((d > 0) & (l + d < line))
            def _():
                source = across + 2 * d
                down(source, m).wait_recv()

                @pl.when(l > 0)
                def _():
                    down(source, m).start()

        return i

    def drain(b, j):
        source = 2 * b + y
        other = 2 * b + 1 - y

        @pl.when((l < line - 1) & (b <= l))
        def _():
            up(source, j).wait_send()

            @pl.when(cross_chunk(j))
            def _():
                up(other, j).wait_send()

        @pl.when((l > 0) & (b >= l))
        def _():
            down(source, j).wait_send()

            @pl.when(cross_chunk(j))
            def _():
                down(other, j).wait_send()

        @pl.when((b == l) | jnp.logical_not(cross_chunk(j)))
        def _():
            side(source, j).wait_send()

        return j

    def multiply(lhs, block):
        w = dense[pl.ds(pl.multiple_of(block * cols, cols), cols), :]
        return lax.dot_general(lhs, w, (((1,), (1,)), ((), ())), preferred_element_type=jnp.float32)

    def main(i, carry):
        @pl.when(i + AHEAD < nc)
        def _():
            send_own(i + AHEAD)

        lax.fori_loop(0, line, forward, i)

        j = i - latest

        @pl.when(inside(j))
        def _():
            @pl.when(jnp.logical_not(cross_chunk(j)))
            def _():
                def arrived(b, carry):
                    side(2 * b + 1 - y, j).wait_recv()
                    return carry

                lax.fori_loop(0, line, arrived, 0)

            span = pl.ds(pl.multiple_of(j * rc, rc), rc)
            lhs = jnp.concatenate([gat[b, span, :] for b in range(nt)], axis=1)
            for m in range(nh):
                give[j, m] = multiply(lhs, 2 * m + 1 - c)
            core_copy(j).start()
            for m in range(nh):
                keep[j, m] = multiply(lhs, 2 * lax.rem(h + m, nh) + c)

        k = j - 1

        @pl.when(inside(k))
        def _():
            core_copy(k).wait_recv()
            for m in range(1, nh):
                x_out[k, m - 1] = keep[k, m] + core_in[k, lax.rem(h + m, nh)]
                x_copy(k, m).start()

        n = j - 2

        @pl.when(inside(n))
        def _():
            total = keep[n, 0] + core_in[n, h]
            for m in range(1, nh):
                x_copy(n, m).wait_recv()
                total = total + x_in[n, m - 1]
            span = pl.ds(pl.multiple_of(n * rc, rc), rc)
            residual = src_v[span, :] + total
            res_v[span, :] = residual
            step = residual / (virt[...] - occ_col[span, :])
            step_v[span, :] = step
            square = jnp.sum((step * step).reshape(rc // 8, 8, cols), axis=0)
            part = square[:, :BT]
            for m in range(1, q):
                part = part + square[:, m * BT : (m + 1) * BT]
            sq[...] += part
            res_copy(n).start()

            @pl.when(n < nc - 1)
            def _():
                lax.fori_loop(0, line, drain, n)
                core_copy(n).wait_send()
                for m in range(1, nh):
                    x_copy(n, m).wait_send()

        return carry

    lax.fori_loop(0, nc + latest + 2, main, 0)

    def stat_rep(m):
        return pltpu.make_async_remote_copy(
            src_ref=sq, dst_ref=stat_a.at[m - 1], send_sem=sas.at[m - 1], recv_sem=sar.at[m - 1],
            device_id={"rep": lax.rem(r + m, nr)}, device_id_type=MESH,
        )

    def stat_tile(m):
        return pltpu.make_async_remote_copy(
            src_ref=mine, dst_ref=stat_b.at[m - 1], send_sem=sbs.at[m - 1], recv_sem=sbr.at[m - 1],
            device_id={"tile": lax.rem(t + m, nt)}, device_id_type=MESH,
        )

    for m in range(1, nr):
        stat_rep(m).start()
    total = sq[...]
    for m in range(1, nr):
        stat_rep(m).wait_recv()
        total = total + stat_a[m - 1]
    mine[...] = total
    for m in range(1, nt):
        stat_tile(m).start()
    for m in range(1, nt):
        stat_tile(m).wait_recv()
        total = total + stat_b[m - 1]
    mean = jnp.sum(total, keepdims=True) / (rows_all * cols * nt * nr)
    scale = jnp.minimum(1.0, trust / jnp.sqrt(mean + 1e-06))

    def finish(j, carry):
        span = pl.ds(pl.multiple_of(j * rc, rc), rc)
        step_v[span, :] = gat[t, span, :].astype(jnp.float32) + scale * step_v[span, :]
        pltpu.make_async_copy(step_v.at[span], upd_out.at[span], usem.at[j]).start()
        return carry

    lax.fori_loop(0, nc, finish, 0)

    lax.fori_loop(0, line, drain, nc - 1)
    core_copy(nc - 1).wait_send()
    for m in range(1, nh):
        x_copy(nc - 1, m).wait_send()
    for m in range(1, nr):
        stat_rep(m).wait_send()
    for m in range(1, nt):
        stat_tile(m).wait_send()

    def written(j, carry):
        span = pl.ds(pl.multiple_of(j * rc, rc), rc)
        res_copy(j).wait()
        pltpu.make_async_copy(step_v.at[span], upd_out.at[span], usem.at[j]).wait()
        return carry

    lax.fori_loop(0, nc, written, 0)


def local(nt, nr, amplitudes, integrals, slot_row, slot_col, slot_count, source, occ_energy, virt_energy):
    rows, cols = amplitudes.shape
    nloc = integrals.shape[1]
    nc = CHUNKS
    rc = rows // nc
    nh = nr // 2
    qr = nt * (cols // BT)
    pairs = PT_DEV * qr
    f32 = jnp.float32
    dma = pltpu.SemaphoreType.DMA
    vmem = pl.BlockSpec(memory_space=pltpu.VMEM)
    anywhere = pl.BlockSpec(memory_space=pl.ANY)
    scratch = [
        pltpu.VMEM((nt, rows, cols), jnp.bfloat16),
        pltpu.VMEM((nloc + 1, BT, BT), jnp.bfloat16),
        pltpu.VMEM((PT_DEV * BT, nt * cols), jnp.bfloat16),
        pltpu.VMEM((8, pairs), jnp.int32),
        pltpu.SMEM((8, pairs), jnp.int32),
        pltpu.VMEM((rows, 1), f32),
        pltpu.VMEM((nc, nh, rc, cols), f32),
        pltpu.VMEM((nc, nh, rc, cols), f32),
        pltpu.VMEM((nc, nh, rc, cols), f32),
        pltpu.VMEM((nc, nh - 1, rc, cols), f32),
        pltpu.VMEM((nc, nh - 1, rc, cols), f32),
        pltpu.VMEM((rows, cols), f32),
        pltpu.VMEM((rows, cols), f32),
        pltpu.VMEM((rows, cols), f32),
        pltpu.VMEM((8, BT), f32),
        pltpu.VMEM((nr - 1, 8, BT), f32),
        pltpu.VMEM((nt - 1, 8, BT), f32),
        pltpu.VMEM((8, BT), f32),
        dma((nt, nc)), dma((nt, nc)), dma((nt, nc)), dma((nt, nc)),
        dma((nc,)), dma((nc,)), dma((nc, nh - 1)), dma((nc, nh - 1)),
        dma((nr - 1,)), dma((nr - 1,)), dma((nt - 1,)), dma((nt - 1,)),
        dma((4,)), dma((nc,)), dma((nc,)),
    ]
    out = jax.ShapeDtypeStruct((rows, cols), f32)
    return pl.pallas_call(
        functools.partial(kernel, nt, nr, nc),
        out_shape=(out, out),
        in_specs=[anywhere, anywhere, vmem, vmem, vmem, anywhere, vmem, vmem],
        out_specs=(anywhere, anywhere),
        scratch_shapes=scratch,
        compiler_params=pltpu.CompilerParams(
            collective_id=0, has_side_effects=True, vmem_limit_bytes=61 * 1024 * 1024
        ),
        name="ladder",
    )(
        amplitudes, integrals, slot_row, slot_col, slot_count, source,
        occ_energy.reshape(1, rows), virt_energy.reshape(1, cols),
    )


def solution(mesh):
    placed = (
        P(None, ("tile", "rep")),
        P("rep", "tile", None, None),
        P("rep", "tile"),
        P("rep", "tile"),
        P("rep", "tile"),
        P(None, ("tile", "rep")),
        P(),
        P(("tile", "rep")),
    )
    return jax.shard_map(
        functools.partial(local, mesh.shape["tile"], mesh.shape["rep"]),
        mesh=mesh,
        in_specs=placed,
        out_specs=(P(None, ("tile", "rep")), P(None, ("tile", "rep"))),
        check_vma=False,
    )
```

time: 286 us -> 90.3 us (0.32)
  waiting for transfers between devices: 142 us -> 0 us
  Pallas kernels: 0 us -> 85.5 us
  matrix products: 50.4 us -> 0 us
  blocking collectives: 39.4 us -> 0 us
  local copies, waits for them, and re-layouts: 31.8 us -> 3.32 us
  between operations: 15.4 us -> 1.29 us
  other arithmetic: 5.65 us -> 0 us
    pallas_call x0 -> x1, Pallas kernels: none -> 85.5 us  [local(): pl.pallas_call(functools.partial(kernel, nt, nr, nc), out_shape=(out, out...]
    all_gather x1 -> x0, waiting for transfers between devices: 76.2 us -> none  [local(): gathered = lax.all_gather(amplitudes, 'tile', axis=1, tiled=True)]
    reduce_scatter x1 -> x0, waiting for transfers between devices: 65.9 us -> none  [local(): lax.psum_scatter(partial_value, 'rep', scatter_dimension=1, tiled=True)]
    dot_general x6 -> x0, matrix products: 50.4 us -> none  [the longest x3 39.6 us: add_block(): jnp.einsum('sk,soe->oke', select, terms, precision=lax.Precision.HIGHEST)]
    psum x1 -> x0, blocking collectives: 39.4 us -> none  [local(): total_sq = lax.psum(jnp.sum(step * step), ('tile', 'rep'))]
    gather x3 -> x0, local copies, waits for them, and re-layouts: 15.7 us -> none  [add_block(): picked = jnp.take(tiles, cblock, axis=1)]
    while x1 -> x0, local copies, waits for them, and re-layouts: 6.38 us -> none  [slot_terms(): total = lax.fori_loop(lower, upper, add_block, total)]
    unnamed x16 -> x4, local copies, waits for them, and re-layouts: 7.2 us -> 3.32 us
  transfers between devices with their start and end apart: 2 -> 0, of which waited for: 2 -> 0; matrix products, arithmetic and copies ran while one was open for 0% -> 0% of each run, Pallas kernels for 0% -> 0%
where the time goes in v1:
time: 90.3 us; the launch traced here: 90.2 us
  Pallas kernels  85.5 us (95%)
  local copies, waits for them, and re-layouts  3.32 us (4%)
  between operations  1.29 us (1%)
    pallas_call x1, Pallas kernels, local(): pl.pallas_call(functools.partial(kernel, nt, nr, nc), out_shape=(out, out...  85.5 us
    unnamed x4, local copies, waits for them, and re-layouts  3.32 us

profile of v1, /device:TPU:0, one launch (start us, length us, event | category | flops | bytes accessed | tf_op | source)
XLA Modules:
  0.0 90.2 jit_solution(2057986472123285883)
XLA Ops:
  1.3 85.5 %ladder.1 = (f32[1024,256]{1,0:T(8,128)}, f32[1024,256]{1,0:T(8,128)}) custom-call(bf16[1024,256]{1,0:T(8,128)(2,1)} %amp.1, bf16[1,64,128,128]{3,2,1,0:T(8,128)(2,1)} %ints.1, s32[1,64]{1,0:T(1,128)} %row.1, s32[1,64]{1,0:T(1,128)} %col.1, s32[1,1]{1,0:T(1,128)S(6)} %copy.12.cnt, f32[1024,256]{1,0:T(8,128)} %src.1, f32[1,1024]{1,0:T(1,128)} %bitcast.2, ...), custom_call_target="tpu_custom_call" | custom-call | tf_op jit(solution)/shard_map/ladder/pallas_call | solution.py:400
  86.8 0.0 copy-start
  86.8 2.4 %copy.13 = f32[1024,256]{1,0:T(8,128)} copy(f32[1024,256]{1,0:T(8,128)} %get-tuple-element.4) | data formatting | bytes 2097152
  89.2 0.0 copy-done
  89.2 1.0 %copy.14 = f32[1024,256]{1,0:T(8,128)} copy(f32[1024,256]{1,0:T(8,128)S(1)} %copy-done) | data formatting | bytes 2097152
Async XLA Ops:
  86.8 2.4 %copy-start = (f32[1024,256]{1,0:T(8,128)S(1)}, f32[1024,256]{1,0:T(8,128)}, u32[]{:S(2)}) copy-start(f32[1024,256]{1,0:T(8,128)} %get-tuple-element.5) | copy-start | bytes 3145732

commit v2 on v1

--- a/solution.py
+++ b/solution.py
@@ -10,22 +10,22 @@
 BT = 128
 PT_DEV = 8
 trust = 0.1
-CHUNKS = 16
+CHUNKS = 8
 AHEAD = 4
 MESH = pl.DeviceIdType.MESH
 
 
 def cross_chunk(j):
-    return lax.rem(j, 5) == 2
+    return lax.rem(j, 8) == 3
 
 
 def kernel(
     nt, nr, nc,
     amp, ints, row, col, cnt, src, occ, virt,
-    res_out, upd_out,
-    gat, tiles, dense, inv_v, inv_s, occ_col, give, keep, core_in, x_out, x_in, src_v, res_v, step_v,
+    lad_out, scale_out,
+    gat, tiles, dense, inv_v, inv_s, occ_col, give, keep, core_in, x_out, x_in, src_v, lad_v,
     sq, stat_a, stat_b, mine,
-    su, sd, sy, rg, ds_, dr, xs, xr, sas, sar, sbs, sbr, loc, rsem, usem,
+    su, sd, sy, rg, ds_, dr, xs, xr, sas, sar, sbs, sbr, loc, rsem,
 ):
     t = lax.axis_index("tile")
     r = lax.axis_index("rep")
@@ -122,9 +122,9 @@
     lax.fori_loop(0, nt, build, 0)
     src_in.wait()
 
-    def core_copy(j):
+    def core_copy(j, m):
         return pltpu.make_async_remote_copy(
-            src_ref=give.at[j], dst_ref=core_in.at[j], send_sem=ds_.at[j], recv_sem=dr.at[j],
+            src_ref=give.at[j, m], dst_ref=core_in.at[j, m], send_sem=ds_.at[j, m], recv_sem=dr.at[j, m],
             device_id={"rep": r + 1 - 2 * c}, device_id_type=MESH,
         )
 
@@ -134,9 +134,9 @@
             device_id={"rep": lax.rem(h + m, nh) * 2 + c}, device_id_type=MESH,
         )
 
-    def res_copy(j):
+    def lad_copy(j):
         span = pl.ds(pl.multiple_of(j * rc, rc), rc)
-        return pltpu.make_async_copy(res_v.at[span], res_out.at[span], rsem.at[j])
+        return pltpu.make_async_copy(lad_v.at[span], lad_out.at[span], rsem.at[j])
 
     latest = line
 
@@ -261,51 +261,48 @@
 
             span = pl.ds(pl.multiple_of(j * rc, rc), rc)
             lhs = jnp.concatenate([gat[b, span, :] for b in range(nt)], axis=1)
-            for m in range(nh):
-                give[j, m] = multiply(lhs, 2 * m + 1 - c)
-            core_copy(j).start()
-            for m in range(nh):
+            order = list(range(1, nh)) + [0]
+            for m in order:
+                give[j, m] = multiply(lhs, 2 * lax.rem(h + m, nh) + 1 - c)
+                core_copy(j, m).start()
+            for m in order:
                 keep[j, m] = multiply(lhs, 2 * lax.rem(h + m, nh) + c)
-
-        k = j - 1
-
-        @pl.when(inside(k))
-        def _():
-            core_copy(k).wait_recv()
             for m in range(1, nh):
-                x_out[k, m - 1] = keep[k, m] + core_in[k, lax.rem(h + m, nh)]
-                x_copy(k, m).start()
-
-        n = j - 2
+                core_copy(j, m).wait_recv()
+                x_out[j, m - 1] = keep[j, m] + core_in[j, m]
+                x_copy(j, m).start()
+
+        n = j - 1
 
         @pl.when(inside(n))
         def _():
-            total = keep[n, 0] + core_in[n, h]
+            core_copy(n, 0).wait_recv()
+            total = keep[n, 0] + core_in[n, 0]
             for m in range(1, nh):
                 x_copy(n, m).wait_recv()
                 total = total + x_in[n, m - 1]
             span = pl.ds(pl.multiple_of(n * rc, rc), rc)
             residual = src_v[span, :] + total
-            res_v[span, :] = residual
+            lad_v[span, :] = total
+            lad_copy(n).start()
             step = residual / (virt[...] - occ_col[span, :])
-            step_v[span, :] = step
             square = jnp.sum((step * step).reshape(rc // 8, 8, cols), axis=0)
             part = square[:, :BT]
             for m in range(1, q):
                 part = part + square[:, m * BT : (m + 1) * BT]
             sq[...] += part
-            res_copy(n).start()
 
             @pl.when(n < nc - 1)
             def _():
                 lax.fori_loop(0, line, drain, n)
-                core_copy(n).wait_send()
+                for m in range(nh):
+                    core_copy(n, m).wait_send()
                 for m in range(1, nh):
                     x_copy(n, m).wait_send()
 
         return carry
 
-    lax.fori_loop(0, nc + latest + 2, main, 0)
+    lax.fori_loop(0, nc + latest + 1, main, 0)
 
     def stat_rep(m):
         return pltpu.make_async_remote_copy(
@@ -322,42 +319,35 @@
     for m in range(1, nr):
         stat_rep(m).start()
     total = sq[...]
+
+    lax.fori_loop(0, line, drain, nc - 1)
+    for m in range(nh):
+        core_copy(nc - 1, m).wait_send()
+    for m in range(1, nh):
+        x_copy(nc - 1, m).wait_send()
+
     for m in range(1, nr):
         stat_rep(m).wait_recv()
         total = total + stat_a[m - 1]
     mine[...] = total
     for m in range(1, nt):
         stat_tile(m).start()
+
+    def written(j, carry):
+        lad_copy(j).wait()
+        return carry
+
+    lax.fori_loop(0, nc, written, 0)
+    for m in range(1, nr):
+        stat_rep(m).wait_send()
     for m in range(1, nt):
         stat_tile(m).wait_recv()
         total = total + stat_b[m - 1]
     mean = jnp.sum(total, keepdims=True) / (rows_all * cols * nt * nr)
     scale = jnp.minimum(1.0, trust / jnp.sqrt(mean + 1e-06))
-
-    def finish(j, carry):
-        span = pl.ds(pl.multiple_of(j * rc, rc), rc)
-        step_v[span, :] = gat[t, span, :].astype(jnp.float32) + scale * step_v[span, :]
-        pltpu.make_async_copy(step_v.at[span], upd_out.at[span], usem.at[j]).start()
-        return carry
-
-    lax.fori_loop(0, nc, finish, 0)
-
-    lax.fori_loop(0, line, drain, nc - 1)
-    core_copy(nc - 1).wait_send()
-    for m in range(1, nh):
-        x_copy(nc - 1, m).wait_send()
-    for m in range(1, nr):
-        stat_rep(m).wait_send()
+    scale_out[...] = jnp.broadcast_to(scale, scale_out.shape)
     for m in range(1, nt):
         stat_tile(m).wait_send()
-
-    def written(j, carry):
-        span = pl.ds(pl.multiple_of(j * rc, rc), rc)
-        res_copy(j).wait()
-        pltpu.make_async_copy(step_v.at[span], upd_out.at[span], usem.at[j]).wait()
-        return carry
-
-    lax.fori_loop(0, nc, written, 0)
 
 
 def local(nt, nr, amplitudes, integrals, slot_row, slot_col, slot_count, source, occ_energy, virt_energy):
@@ -386,31 +376,32 @@
         pltpu.VMEM((nc, nh - 1, rc, cols), f32),
         pltpu.VMEM((rows, cols), f32),
         pltpu.VMEM((rows, cols), f32),
-        pltpu.VMEM((rows, cols), f32),
         pltpu.VMEM((8, BT), f32),
         pltpu.VMEM((nr - 1, 8, BT), f32),
         pltpu.VMEM((nt - 1, 8, BT), f32),
         pltpu.VMEM((8, BT), f32),
         dma((nt, nc)), dma((nt, nc)), dma((nt, nc)), dma((nt, nc)),
-        dma((nc,)), dma((nc,)), dma((nc, nh - 1)), dma((nc, nh - 1)),
+        dma((nc, nh)), dma((nc, nh)), dma((nc, nh - 1)), dma((nc, nh - 1)),
         dma((nr - 1,)), dma((nr - 1,)), dma((nt - 1,)), dma((nt - 1,)),
-        dma((4,)), dma((nc,)), dma((nc,)),
+        dma((4,)), dma((nc,)),
     ]
-    out = jax.ShapeDtypeStruct((rows, cols), f32)
-    return pl.pallas_call(
+    ladder, scale = pl.pallas_call(
         functools.partial(kernel, nt, nr, nc),
-        out_shape=(out, out),
+        out_shape=(jax.ShapeDtypeStruct((rows, cols), f32), jax.ShapeDtypeStruct((1, cols), f32)),
         in_specs=[anywhere, anywhere, vmem, vmem, vmem, anywhere, vmem, vmem],
-        out_specs=(anywhere, anywhere),
+        out_specs=(anywhere, vmem),
         scratch_shapes=scratch,
         compiler_params=pltpu.CompilerParams(
-            collective_id=0, has_side_effects=True, vmem_limit_bytes=61 * 1024 * 1024
+            collective_id=0, has_side_effects=True, vmem_limit_bytes=60 * 1024 * 1024
         ),
         name="ladder",
     )(
         amplitudes, integrals, slot_row, slot_col, slot_count, source,
         occ_energy.reshape(1, rows), virt_energy.reshape(1, cols),
     )
+    residual = source + ladder
+    step = residual / (virt_energy[None, :] - occ_energy[:, None])
+    return residual, amplitudes.astype(f32) + scale * step
 
 
 def solution(mesh):

time: 90.3 us -> 78.5 us (0.87)
  Pallas kernels: 85.5 us -> 74 us
  local copies, waits for them, and re-layouts: 3.32 us -> 0.02 us
  other arithmetic: 0 us -> 2.84 us
    pallas_call x1, Pallas kernels: 85.5 us -> 74 us  [local(): pl.pallas_call(functools.partial(kernel, nt, nr, nc), out_shape=(jax.Shap...]
    unnamed x4 -> x8, local copies, waits for them, and re-layouts: 3.32 us -> 0.02 us
    add x0 -> x1, other arithmetic: none -> 2.84 us  [local(): return (residual, amplitudes.astype(f32) + scale * step)]
where the time goes in v2:
time: 78.5 us; the launch traced here: 78.4 us
  Pallas kernels  74 us (94%)
  other arithmetic  2.84 us (4%)
  between operations  1.47 us (2%)
    pallas_call x1, Pallas kernels, local(): pl.pallas_call(functools.partial(kernel, nt, nr, nc), out_shape=(jax.Shap...  74 us
    add x1, other arithmetic, local(): return (residual, amplitudes.astype(f32) + scale * step)  2.84 us

profile of v2, /device:TPU:0, one launch (start us, length us, event | category | flops | bytes accessed | tf_op | source)
XLA Modules:
  0.0 78.4 jit_solution(10332022508471877846)
XLA Ops:
  0.6 0.0 copy-start.3
  0.6 0.0 copy-start.2
  0.7 0.0 copy-start
  0.7 0.0 copy-start.1
  1.4 74.0 %ladder.1 = (f32[1024,256]{1,0:T(8,128)}, f32[1,256]{1,0:T(1,128)}) custom-call(bf16[1024,256]{1,0:T(8,128)(2,1)} %amp.1, bf16[1,64,128,128]{3,2,1,0:T(8,128)(2,1)} %ints.1, s32[1,64]{1,0:T(1,128)} %row.1, s32[1,64]{1,0:T(1,128)} %col.1, s32[1,1]{1,0:T(1,128)S(6)} %copy.10.cnt, f32[1024,256]{1,0:T(8,128)} %src.1, f32[1,1024]{1,0:T(1,128)} %bitcast.3, ...), custom_call_target="tpu_custom_call" | custom-call | tf_op jit(solution)/shard_map/ladder/pallas_call | solution.py:388
  75.5 0.0 copy-done.3
  75.5 0.0 copy-done.2
  75.5 0.0 copy-done
  75.5 0.0 copy-done.1
  75.5 2.8 %multiply_add_fusion = (f32[1024,256]{1,0:T(8,128)}, f32[1024,256]{1,0:T(8,128)}) fusion(bf16[1024,256]{1,0:T(8,128)(2,1)S(1)} %copy-done.1, f32[1024]{0:T(1024)S(1)} %copy-done.2, f32[256]{0:T(256)S(1)} %copy-done.3, f32[256]{0:T(256)} %bitcast.5, f32[1024,256]{1,0:T(8,128)S(1)} %copy-done, f32[1024,256]{1,0:T(8,128)} %get-tuple-element.4), kind=kLoop, calls=%fused_computation | loop fusion | flops 1572864 | bytes 4724736 | tf_op jit(solution)/shard_map/add | solution.py:404
Async XLA Ops:
  0.6 74.8 %copy-start.3 = (f32[256]{0:T(256)S(1)}, f32[256]{0:T(256)}, u32[]{:S(2)}) copy-start(f32[256]{0:T(256)} %param.15) | copy-start | bytes 3076
  0.6 74.8 %copy-start.2 = (f32[1024]{0:T(1024)S(1)}, f32[1024]{0:T(1024)}, u32[]{:S(2)}) copy-start(f32[1024]{0:T(1024)} %param.14) | copy-start | bytes 12292
  0.7 74.8 %copy-start = (f32[1024,256]{1,0:T(8,128)S(1)}, f32[1024,256]{1,0:T(8,128)}, u32[]{:S(2)}) copy-start(f32[1024,256]{1,0:T(8,128)} %src.1) | copy-start | bytes 3145732
  0.7 74.8 %copy-start.1 = (bf16[1024,256]{1,0:T(8,128)(2,1)S(1)}, bf16[1024,256]{1,0:T(8,128)(2,1)}, u32[]{:S(2)}) copy-start(bf16[1024,256]{1,0:T(8,128)(2,1)} %amp.1) | copy-start | bytes 1572868

commit v3 on v2

--- a/solution.py
+++ b/solution.py
@@ -16,7 +16,7 @@
 
 
 def cross_chunk(j):
-    return lax.rem(j, 8) == 3
+    return lax.rem(j, 8) == 7
 
 
 def kernel(
@@ -138,7 +138,7 @@
         span = pl.ds(pl.multiple_of(j * rc, rc), rc)
         return pltpu.make_async_copy(lad_v.at[span], lad_out.at[span], rsem.at[j])
 
-    latest = line
+    latest = line - 1
 
     def inside(j):
         return (j >= 0) & (j < nc)

time: 78.5 us -> 77.3 us (0.985)
  Pallas kernels: 74 us -> 72.8 us
    pallas_call x1, Pallas kernels: 74 us -> 72.8 us  [local(): pl.pallas_call(functools.partial(kernel, nt, nr, nc), out_shape=(jax.Shap...]
where the time goes in v3:
time: 77.3 us; the launch traced here: 77.2 us
  Pallas kernels  72.8 us (94%)
  other arithmetic  2.84 us (4%)
  between operations  1.47 us (2%)
    pallas_call x1, Pallas kernels, local(): pl.pallas_call(functools.partial(kernel, nt, nr, nc), out_shape=(jax.Shap...  72.8 us
    add x1, other arithmetic, local(): return (residual, amplitudes.astype(f32) + scale * step)  2.84 us

profile of v3, /device:TPU:0, one launch (start us, length us, event | category | flops | bytes accessed | tf_op | source)
XLA Modules:
  0.0 77.2 jit_solution(6375041705625115990)
XLA Ops:
  0.6 0.0 copy-start.3
  0.6 0.0 copy-start.2
  0.7 0.0 copy-start
  0.7 0.0 copy-start.1
  1.4 72.8 %ladder.1 = (f32[1024,256]{1,0:T(8,128)}, f32[1,256]{1,0:T(1,128)}) custom-call(bf16[1024,256]{1,0:T(8,128)(2,1)} %amp.1, bf16[1,64,128,128]{3,2,1,0:T(8,128)(2,1)} %ints.1, s32[1,64]{1,0:T(1,128)} %row.1, s32[1,64]{1,0:T(1,128)} %col.1, s32[1,1]{1,0:T(1,128)S(6)} %copy.10.cnt, f32[1024,256]{1,0:T(8,128)} %src.1, f32[1,1024]{1,0:T(1,128)} %bitcast.3, ...), custom_call_target="tpu_custom_call" | custom-call | tf_op jit(solution)/shard_map/ladder/pallas_call | solution.py:388
  74.3 0.0 copy-done.3
  74.3 0.0 copy-done.2
  74.3 0.0 copy-done
  74.3 0.0 copy-done.1
  74.3 2.8 %multiply_add_fusion = (f32[1024,256]{1,0:T(8,128)}, f32[1024,256]{1,0:T(8,128)}) fusion(bf16[1024,256]{1,0:T(8,128)(2,1)S(1)} %copy-done.1, f32[1024]{0:T(1024)S(1)} %copy-done.2, f32[256]{0:T(256)S(1)} %copy-done.3, f32[256]{0:T(256)} %bitcast.5, f32[1024,256]{1,0:T(8,128)S(1)} %copy-done, f32[1024,256]{1,0:T(8,128)} %get-tuple-element.4), kind=kLoop, calls=%fused_computation | loop fusion | flops 1572864 | bytes 4724736 | tf_op jit(solution)/shard_map/add | solution.py:404
Async XLA Ops:
  0.6 73.6 %copy-start.3 = (f32[256]{0:T(256)S(1)}, f32[256]{0:T(256)}, u32[]{:S(2)}) copy-start(f32[256]{0:T(256)} %param.15) | copy-start | bytes 3076
  0.6 73.6 %copy-start.2 = (f32[1024]{0:T(1024)S(1)}, f32[1024]{0:T(1024)}, u32[]{:S(2)}) copy-start(f32[1024]{0:T(1024)} %param.14) | copy-start | bytes 12292
  0.7 73.6 %copy-start = (f32[1024,256]{1,0:T(8,128)S(1)}, f32[1024,256]{1,0:T(8,128)}, u32[]{:S(2)}) copy-start(f32[1024,256]{1,0:T(8,128)} %src.1) | copy-start | bytes 3145732
  0.7 73.6 %copy-start.1 = (bf16[1024,256]{1,0:T(8,128)(2,1)S(1)}, bf16[1024,256]{1,0:T(8,128)(2,1)}, u32[]{:S(2)}) copy-start(bf16[1024,256]{1,0:T(8,128)(2,1)} %amp.1) | copy-start | bytes 1572868
